TPU v7x, 256 devices: a whole 4x4x8 slice. The times are simulated.
256 devices in a mesh: fsdp: 64 (over z, y_lo, x), rep: 4 (over y_hi, core).
Axes of the slice: x: 4, y: 4 (y_hi: 2, y_lo: 2; y = y_hi * 2 + y_lo), z: 8, core: 2. Of those that a mesh axis runs over, the one named last changes fastest.
Arguments:
- cross_base: bfloat16 [32768, 4096], P(('fsdp', 'rep')), may hold values from -6 to 6
- layer_in: bfloat16 [32768, 4096], P(('fsdp', 'rep')), may hold values from -6 to 6
- grad_out: bfloat16 [32768, 4096], P(('fsdp', 'rep')), may hold values from -24 to 24
- reduce_a: bfloat16 [4096, 256], P('fsdp'), may hold values from -0.09375 to 0.09375
- expand_a: bfloat16 [4096, 256], P('fsdp'), may hold values from -0.375 to 0.375
- reduce_b: bfloat16 [4096, 256], P('fsdp'), may hold values from -0.09375 to 0.09375
- expand_b: bfloat16 [4096, 256], P('fsdp'), may hold values from -0.375 to 0.375
Outputs:
- grad_layer_in: bfloat16 [32768, 4096], P(('fsdp', 'rep'))
- grad_base: bfloat16 [32768, 4096], P(('fsdp', 'rep'))
- grad_reduce_a: float32 [4096, 256], P('fsdp')
- grad_expand_a: float32 [4096, 256], P('fsdp')
- grad_reduce_b: float32 [4096, 256], P('fsdp')
- grad_expand_b: float32 [4096, 256], P('fsdp')
All inputs are finite; a program needn't handle non-finite values.
Results may differ from a plain program's by a relative error of at most 0.015.
Values may be sent and summed in bfloat16 or wider, within the bound.
A program may use at most 128 MiB of HBM per device.

v0:
```python
import math

import jax
import jax.numpy as jnp
from jax import lax
from jax.sharding import PartitionSpec as P


def in_blocks(value, dim, length):
    dims = value.shape
    pieces = value.reshape(*dims[:dim], length, dims[dim] // length, *dims[dim + 1 :])
    return jnp.moveaxis(pieces, dim, 0)


def sum_at_owner(value, axis, dim):
    pieces = in_blocks(value, dim, lax.axis_size(axis))
    arrived = lax.all_to_all(pieces, axis, split_axis=0, concat_axis=0, tiled=True)
    return arrived.astype(jnp.float32).sum(axis=0)


def sent_to_all(value, axis):
    copies = jnp.broadcast_to(value, (lax.axis_size(axis), *value.shape))
    return lax.all_to_all(copies, axis, split_axis=0, concat_axis=0, tiled=True)


def taken_together(value, axis):
    return sent_to_all(value, axis).astype(jnp.float32).sum(axis=0)


def in_one_piece(arrays, axis, dim, along):
    both = jnp.concatenate(arrays, axis=along)
    out, at, outs = (lax.all_gather(both, axis, axis=dim, tiled=True), 0, [])
    for a in arrays:
        outs.append(lax.slice_in_dim(out, at, at + a.shape[along], axis=along))
        at += a.shape[along]
    return tuple(outs)


def contract_rows(left, right):
    return lax.dot_general(
        left, right, (((0,), (0,)), ((), ())), preferred_element_type=jnp.float32
    )


def contract_cols(left, right):
    return lax.dot_general(
        left, right, (((1,), (1,)), ((), ())), preferred_element_type=jnp.float32
    )


def project(inputs, reduce_full, expand_full):
    narrow = jnp.dot(inputs, reduce_full, preferred_element_type=jnp.float32).astype(jnp.bfloat16)
    return (narrow, contract_cols(narrow, expand_full))


def local_backward(grad_in, cross_base, reduce_full, expand_full):
    grad_wide = grad_in.astype(jnp.float32)
    masked = (grad_wide * cross_base.astype(jnp.float32)).astype(jnp.bfloat16)
    narrow_grad = jnp.dot(masked, expand_full, preferred_element_type=jnp.float32).astype(
        jnp.bfloat16
    )
    passed = grad_wide + contract_cols(narrow_grad, reduce_full)
    return (masked, narrow_grad, passed)


def weight_grads(masked, narrow, inputs, narrow_grad, factor):
    summed = sum_at_owner(
        jnp.concatenate(
            (contract_rows(inputs, narrow_grad), contract_rows(masked, narrow)), axis=1
        ).astype(jnp.bfloat16),
        "fsdp",
        0,
    )
    summed = taken_together(summed.astype(jnp.bfloat16), "rep").astype(jnp.float32)
    summed = summed * factor
    rank_width = narrow.shape[1]
    return (summed[:, :rank_width], summed[:, rank_width:])


def on_device(cross_base, layer_in, grad_out, reduce_a, expand_a, reduce_b, expand_b):
    sample_rows = cross_base.shape[0]
    factor = 1.0 / math.sqrt(sample_rows * lax.axis_size("fsdp") * lax.axis_size("rep"))
    reduce_full, expand_full = in_one_piece((reduce_a, expand_a), "fsdp", 0, 1)
    narrow_a, cross_a = project(layer_in, reduce_full, expand_full)
    base_wide = cross_base.astype(jnp.float32)
    middle = (layer_in.astype(jnp.float32) + base_wide * cross_a).astype(jnp.bfloat16)
    top_reduce, top_expand = in_one_piece((reduce_b, expand_b), "fsdp", 0, 1)
    narrow_b, cross_b = project(middle, top_reduce, top_expand)
    masked_b, narrow_grad_b, passed_b = local_backward(grad_out, cross_base, top_reduce, top_expand)
    grad_reduce_b, grad_expand_b = weight_grads(masked_b, narrow_b, middle, narrow_grad_b, factor)
    grad_middle = passed_b.astype(jnp.bfloat16)
    masked_a, narrow_grad_a, passed_a = local_backward(
        grad_middle, cross_base, reduce_full, expand_full
    )
    grad_reduce_a, grad_expand_a = weight_grads(masked_a, narrow_a, layer_in, narrow_grad_a, factor)
    grad_layer_in = passed_a.astype(jnp.bfloat16)
    grad_base = (
        grad_out.astype(jnp.float32) * cross_b + grad_middle.astype(jnp.float32) * cross_a
    ).astype(jnp.bfloat16)
    return (grad_layer_in, grad_base, grad_reduce_a, grad_expand_a, grad_reduce_b, grad_expand_b)


def solution(mesh):
    placed = (
        P(("fsdp", "rep"), None),
        P(("fsdp", "rep"), None),
        P(("fsdp", "rep"), None),
        P("fsdp", None),
        P("fsdp", None),
        P("fsdp", None),
        P("fsdp", None),
    )
    return jax.shard_map(
        on_device,
        mesh=mesh,
        in_specs=placed,
        out_specs=(
            P(("fsdp", "rep"), None),
            P(("fsdp", "rep"), None),
            P("fsdp", None),
            P("fsdp", None),
            P("fsdp", None),
            P("fsdp", None),
        ),
        check_vma=False,
    )
```

profile of v0, /device:TPU:1, one launch (start us, length us, event | category | flops | bytes accessed | tf_op | source)
XLA Modules:
  0.0 822.7 jit_solution(10918637260076536532)
XLA Ops:
  7.2 1.4 pad_maximum_fusion.3
  8.7 1.5 pad_maximum_fusion.2
  10.3 261.0 %all-gather.5.cloned.1.call-done = bf16[4096,512]{1,0:T(8,128)(2,1)} async-done(((bf16[64,512]{1,0:T(8,128)(2,1)}), bf16[4096,512]{1,0:T(8,128)(2,1)}) %all-gather.5.cloned.1.call-update) | async-done | bytes 4194320 | tf_op jit(solution)/shard_map/all_gather | solution.py:32
  271.3 2.6 fusion.32
  273.9 4.2 fusion.9
  278.1 296.0 %all-gather.3.cloned.1.call-done = bf16[4096,512]{1,0:T(8,128)(2,1)} async-done(((bf16[64,512]{1,0:T(8,128)(2,1)}), bf16[4096,512]{1,0:T(8,128)(2,1)}) %all-gather.3.cloned.1.call-update) | async-done | bytes 4194320 | tf_op jit(solution)/shard_map/all_gather | solution.py:32
  574.1 2.2 fusion.23
  576.3 0.7 convolution_convert_fusion.1
  577.5 0.8 convolution_convert_fusion
  578.3 2.3 pad_maximum_fusion.1
  580.6 7.9 all-to-all-start.2
  588.6 2.8 fusion.3
  591.7 0.5 fusion.29
  592.2 0.7 copy-done.6
  592.9 2.0 fusion
  595.0 4.1 copy.15
  599.0 0.8 convolution_convert_fusion.2
  599.8 0.8 copy-done.4
  600.6 2.3 pad_maximum_fusion
  602.9 36.2 %all-to-all-done.2 = bf16[64,64,512]{2,1,0:T(8,128)(2,1)} async-done(((bf16[64,64,512]{2,1,0:T(8,128)(2,1)}), bf16[64,64,512]{2,1,0:T(8,128)(2,1)}, u32[]{:S(2)}, u32[]{:S(2)}) %all-to-all-start.2) | async-done | bytes 4194336 | tf_op jit(solution)/shard_map/all_to_all | solution.py:17
  639.2 8.5 %all-to-all-start = ((bf16[64,64,512]{2,1,0:T(8,128)(2,1)}), bf16[64,64,512]{2,1,0:T(8,128)(2,1)}, u32[]{:S(2)}, u32[]{:S(2)}) async-start(bf16[64,64,512]{2,1,0:T(8,128)(2,1)} %pad_maximum_fusion), calls=%async_computation | async-start | bytes 8388608 | tf_op jit(solution)/shard_map/all_to_all | solution.py:17
  647.7 4.0 fusion.5
  651.8 2.8 reduce_sum.44
  654.6 82.6 %all-to-all-done = bf16[64,64,512]{2,1,0:T(8,128)(2,1)} async-done(((bf16[64,64,512]{2,1,0:T(8,128)(2,1)}), bf16[64,64,512]{2,1,0:T(8,128)(2,1)}, u32[]{:S(2)}, u32[]{:S(2)}) %all-to-all-start) | async-done | bytes 4194336 | tf_op jit(solution)/shard_map/all_to_all | solution.py:17
  737.2 0.7 broadcast_in_dim.7
  737.9 58.9 %all-to-all-start.3 = ((bf16[4,64,512]{2,1,0:T(8,128)(2,1)}), bf16[4,64,512]{2,1,0:T(8,128)(2,1)S(1)}, u32[]{:S(2)}, u32[]{:S(2)}) async-start(bf16[4,64,512]{2,1,0:T(8,128)(2,1)} %broadcast_in_dim.7), calls=%async_computation.3 | async-start | bytes 524288 | tf_op jit(solution)/shard_map/all_to_all | solution.py:23
  796.8 3.4 fusion.4
  800.2 2.8 reduce_sum.42
  803.4 0.7 broadcast_in_dim.6
  804.1 4.5 all-to-all-start.1
  808.6 6.5 all-to-all-done.1
  815.2 0.7 fusion.39
  (26 shorter events, 1.3 us)
Async XLA Ops:
  7.2 264.1 %all-gather.5.cloned.1.call-start = ((), (), s32[]{:S(2)}) async-start(), calls=%async_computation.5 | async-start | bytes 4259840 | tf_op jit(solution)/shard_map/all_gather | solution.py:32
  8.6 265.3 %copy-start = (bf16[128,4096]{1,0:T(8,128)(2,1)S(1)}, bf16[128,4096]{1,0:T(8,128)(2,1)}, u32[]{:S(2)}) copy-start(bf16[128,4096]{1,0:T(8,128)(2,1)} %param.7) | copy-start | bytes 3145732
  8.6 265.3 %copy-start.5 = (bf16[128,4096]{1,0:T(8,128)(2,1)S(1)}, bf16[128,4096]{1,0:T(8,128)(2,1)}, u32[]{:S(2)}) copy-start(bf16[128,4096]{1,0:T(8,128)(2,1)} %param.8) | copy-start | bytes 3145732
  8.7 565.4 %all-gather.3.cloned.1.call-start = ((), (), s32[]{:S(2)}) async-start(), calls=%async_computation.4 | async-start | bytes 4259840 | tf_op jit(solution)/shard_map/all_gather | solution.py:32
  273.9 300.2 %copy-start.2 = (bf16[128,4096]{1,0:T(8,128)(2,1)S(1)}, bf16[128,4096]{1,0:T(8,128)(2,1)}, u32[]{:S(2)}) copy-start(bf16[128,4096]{1,0:T(8,128)(2,1)} %param.9) | copy-start | bytes 3145732
  278.1 298.2 %copy-start.7 = (bf16[128,4096]{1,0:T(8,128)(2,1)S(1)}, bf16[128,4096]{1,0:T(8,128)(2,1)}, u32[]{:S(2)}) copy-start(bf16[128,4096]{1,0:T(8,128)(2,1)} %get-tuple-element.10) | copy-start | bytes 3145732
  574.1 3.0 copy-start.8
  580.6 58.6 %all-to-all-start.2 = ((bf16[64,64,512]{2,1,0:T(8,128)(2,1)}), bf16[64,64,512]{2,1,0:T(8,128)(2,1)}, u32[]{:S(2)}, u32[]{:S(2)}) async-start(bf16[64,64,512]{2,1,0:T(8,128)(2,1)} %pad_maximum_fusion.1), calls=%async_computation.2 | async-start | bytes 8388608 | tf_op jit(solution)/shard_map/all_to_all | solution.py:17
  588.5 3.1 copy-start.1
  591.7 1.2 copy-start.6
  599.0 1.6 copy-start.4
  602.9 44.8 %copy-start.3 = (bf16[128,4096]{1,0:T(8,128)(2,1)S(1)}, bf16[128,4096]{1,0:T(8,128)(2,1)}, u32[]{:S(2)}) copy-start(bf16[128,4096]{1,0:T(8,128)(2,1)} %param.9) | copy-start | bytes 3145732
  639.2 98.0 %all-to-all-start = ((bf16[64,64,512]{2,1,0:T(8,128)(2,1)}), bf16[64,64,512]{2,1,0:T(8,128)(2,1)}, u32[]{:S(2)}, u32[]{:S(2)}) async-start(bf16[64,64,512]{2,1,0:T(8,128)(2,1)} %pad_maximum_fusion), calls=%async_computation | async-start | bytes 8388608 | tf_op jit(solution)/shard_map/all_to_all | solution.py:17
  737.9 65.5 %all-to-all-start.3 = ((bf16[4,64,512]{2,1,0:T(8,128)(2,1)}), bf16[4,64,512]{2,1,0:T(8,128)(2,1)S(1)}, u32[]{:S(2)}, u32[]{:S(2)}) async-start(bf16[4,64,512]{2,1,0:T(8,128)(2,1)} %broadcast_in_dim.7), calls=%async_computation.3 | async-start | bytes 524288 | tf_op jit(solution)/shard_map/all_to_all | solution.py:23
  804.1 11.0 %all-to-all-start.1 = ((bf16[4,64,512]{2,1,0:T(8,128)(2,1)}), bf16[4,64,512]{2,1,0:T(8,128)(2,1)S(1)}, u32[]{:S(2)}, u32[]{:S(2)}) async-start(bf16[4,64,512]{2,1,0:T(8,128)(2,1)} %broadcast_in_dim.6), calls=%async_computation.1 | async-start | bytes 524288 | tf_op jit(solution)/shard_map/all_to_all | solution.py:23
Sparse Core Ops, SparseCore 0:
  10.3 260.8 all-gather.4
  273.6 300.3 all-gather.2
where the time goes:
time: 823 us
  waiting for transfers between devices  683 us (83%)
  starting transfers between devices  80 us (10%)
  matrix products  24.5 us (3%)
  between operations  14.2 us (2%)
  other arithmetic  13.4 us (2%)
    all_gather x2, waiting for transfers between devices, in_one_piece(): out, at, outs = (lax.all_gather(both, axis, axis=dim, tiled=True), 0, [])  557 us
    all_to_all x2, waiting for transfers between devices, sum_at_owner(): lax.all_to_all(pieces, axis, split_axis=0, concat_axis=0, tiled=True)  119 us
    all_to_all x2, starting transfers between devices, sent_to_all(): return lax.all_to_all(copies, axis, split_axis=0, concat_axis=0, tiled=True)  63.4 us
    all_to_all x2, starting transfers between devices, sum_at_owner(): lax.all_to_all(pieces, axis, split_axis=0, concat_axis=0, tiled=True)  16.5 us
  transfers between devices with their start and end apart: 6, of which 6 were waited for; matrix products, arithmetic and copies ran while one was open for 4% of the time, Pallas kernels for 0%

commit v1 on v0

v1 whole, which is shorter than its diff:
```python
import functools
import math

import jax
import jax.numpy as jnp
from jax import lax
from jax.experimental import pallas as pl
from jax.experimental.pallas import tpu as pltpu
from jax.sharding import PartitionSpec as P

NX, NY, NZ = 4, 4, 8
ROWS, RANK, PLANE, D, TOK = 64, 256, 512, 4096, 128
HALF = ROWS // 2
BF, F32 = jnp.bfloat16, jnp.float32
FAR = (4, 3, -3, 2, -2, 1, -1, 0)
NEAR = (0, 1, -1, 2, -2, 3, -3, 4)
UP = (0, -1, -2, -3)
R1, R2 = pl.ds(0, HALF), pl.ds(HALF, HALF)
OUTS = 4


class Place:
    def __init__(self):
        f, r = lax.axis_index("fsdp"), lax.axis_index("rep")
        self.z, self.yl, self.x = f // 8, (f // 4) % 2, f % 4
        self.yh, self.c = r // 2, r % 2
        self.y = self.yh * 2 + self.yl
        self.s = 1 - 2 * self.c
        self.oyl = 1 - self.yl
        self.planes = {d: (self.z + self.s * d + NZ) % NZ for d in range(-4, 5)}
        self.cols = {d: (self.x + self.s * d + NX) % NX for d in range(-2, 3)}

    def at(self, x, y, z, c):
        return {"fsdp": (z * 2 + y % 2) * 4 + x, "rep": (y // 2) * 2 + c}

    def dx(self, d):
        return self.at(self.cols[d], self.y, self.z, self.c)

    def dy(self, d):
        return self.at(self.x, (self.y + self.s * d + NY) % NY, self.z, self.c)

    def dz(self, d):
        return self.at(self.x, self.y, self.planes[d], self.c)

    def mate(self):
        return self.at(self.x, self.y, self.z, 1 - self.c)

    def peers(self):
        return (
            [self.dx(d) for d in (1, -1, 2)]
            + [self.dy(d) for d in (1, -1, 2)]
            + [self.dz(d) for d in (1, -1, 2, -2, 3, -3, 4)]
            + [self.mate()]
        )


class Mail:
    def __init__(self, send, recv):
        self.send, self.recv, self.ids, self.live = send, recv, {}, []

    def index(self, key):
        return self.ids.setdefault(key, len(self.ids))

    def put(self, key, src, dst, dev):
        i = self.index(key)
        copy = pltpu.make_async_remote_copy(
            src_ref=src, dst_ref=dst, send_sem=self.send.at[i], recv_sem=self.recv.at[i],
            device_id=dev, device_id_type=pl.DeviceIdType.MESH,
        )
        copy.start()
        self.live.append((key, copy))

    def got(self, key):
        for k, copy in self.live:
            if k == key:
                copy.wait_recv()
                return
        raise KeyError(key)

    def drain(self):
        for _, copy in self.live:
            copy.wait_send()


def gather_events(me, mail, w, p):
    m = 2 * p + me.c
    pn, cn, z, yl, oyl, x = me.planes, me.cols, me.z, me.yl, me.oyl, me.x
    ev = []

    def same(key, ref, dev):
        mail.put((p, 0) + key, ref, ref, dev)

    def got(*key):
        mail.got((p, 0) + key)

    def up(d):
        return 1 if d in UP else -1

    def send_1y(d):
        same(("1y", d), w.at[m, pn[d], yl, :, R1, :], me.dy(up(d)))

    def send_2y(d):
        same(("2y", d), w.at[m, pn[d], yl, x, R2, :], me.dy(up(d)))

    def send_2xa(d):
        for e in (1, -1):
            same(("2xa", d, e), w.at[m, pn[d], :, x, R2, :], me.dx(e))

    def first():
        own1, own2 = w.at[m, z, yl, x, R1, :], w.at[m, z, yl, x, R2, :]
        for d in (2, 1, -1):
            same(("1x", d), own1, me.dx(d))
        send_2y(0)
        for d in (1, -1, 2, -2, 3, -3, 4):
            same(("2z", d), own2, me.dz(d))

    def rows():
        for d in (1, -1, 2):
            got("1x", d)
        for e in (1, -1):
            same(("1z", e, 1), w.at[m, z, yl, :, R1, :], me.dz(e))
        send_1y(0)

    def zs(k):
        for d in ((k, -k) if k < 4 else (4,)):
            got("2z", -d if k < 4 else 4)
            send_2y(d)

    def xa(d):
        got("2y", d)
        send_2xa(d)

    def xb(d):
        for e in (1, -1):
            got("2xa", d, e)
        e = up(d)
        same(("2xb", d), w.at[m, pn[d], :, cn[-e], R2, :], me.dx(e))

    def hop(k):
        for e in (1, -1):
            if (e, k) == (-1, 4):
                continue
            got("1z", e, k)
            d = -e * k
            if k < 3 or (e, k) == (1, 3):
                same(("1z", e, k + 1), w.at[m, pn[d], yl, :, R1, :], me.dz(e))
            send_1y(4 if k == 4 else d)

    def d1(d):
        got("1y", d)
        same(("d1", d), w.at[m, pn[d], :, :, R1, :], me.mate())

    def d2(d):
        got("2xb", d)
        same(("d2", d), w.at[m, pn[d], :, :, R2, :], me.mate())

    def last():
        for d in NEAR:
            got("d1", d)
            got("d2", d)

    ev.append((0.0, first))
    ev.append((3.0, rows))
    ev.append((3.2, functools.partial(zs, 1)))
    ev.append((3.5, functools.partial(xa, 0)))
    ev.append((3.9, functools.partial(zs, 2)))
    ev.append((4.5, functools.partial(zs, 3)))
    ev.append((5.0, functools.partial(zs, 4)))
    for k in range(1, 5):
        t = 4.9 + 0.9 * k
        for d in ((k, -k) if k < 4 else (4,)):
            ev.append((t, functools.partial(xa, d)))
    for k in range(0, 5):
        t = 6.2 + 1.3 * k
        for d in ((k, -k) if 0 < k < 4 else (k,)):
            ev.append((t, functools.partial(xb, d)))
            ev.append((t + 2.6, functools.partial(d2, d)))
    for k in range(1, 5):
        ev.append((3.0 + 3.0 * k, functools.partial(hop, k)))
    for k in range(0, 5):
        t = 6.0 + 3.0 * k
        for d in ((k, -k) if 0 < k < 4 else (k,)):
            ev.append((t, functools.partial(d1, d)))
    ev.append((20.0, last))
    return ev


def scatter_events(me, mail, g, s, dd, st, p, scale):
    m, mo = 2 * p + me.c, 2 * p + 1 - me.c
    pn, cn, z, yl, oyl, x = me.planes, me.cols, me.z, me.yl, me.oyl, me.x
    ev = []
    up_set = (0, 1, 2, 3)

    def up(d):
        return 1 if d in up_set else -1

    def put(key, src, dst, dev):
        mail.put((p, 1) + key, src, dst, dev)

    def got(*key):
        mail.got((p, 1) + key)

    def add(where, *parts):
        tot = s[where]
        for part in parts:
            tot = tot + part
        s[where] = tot

    slot = {d: i for i, d in enumerate(FAR)}

    def swap(d):
        put(("dd", d), g.at[mo, pn[-d]], dd.at[p, pn[-d]], me.mate())

    def send_2xa(d, e):
        put(("2xa", d, e), s.at[p, pn[d], :, cn[e], R2, :], st["xa"].at[p, slot[d], (1 - e) // 2], me.dx(e))

    def join(d):
        got("dd", d)
        s[p, pn[d]] = g[m, pn[d]] + dd[p, pn[d]]
        put(("1y", d), s.at[p, pn[d], oyl, :, R1, :], st["y1"].at[p, slot[d]], me.dy(up(d)))
        put(("2xb", d), s.at[p, pn[d], :, cn[2], R2, :], st["xb"].at[p, slot[d]], me.dx(up(d)))
        send_2xa(d, -up(d))

    def xb(d):
        got("2xb", d)
        e = up(d)
        s[p, pn[d], :, cn[e], R2, :] += st["xb"][p, slot[d]]
        send_2xa(d, e)

    def xa(d):
        for e in (1, -1):
            got("2xa", d, e)
        s[p, pn[d], :, x, R2, :] += st["xa"][p, slot[d], 0] + st["xa"][p, slot[d], 1]
        put(("2y", d), s.at[p, pn[d], oyl, x, R2, :], st["y2"].at[p, slot[d]], me.dy(up(d)))

    def y2(d):
        got("2y", d)
        s[p, pn[d], yl, x, R2, :] += st["y2"][p, slot[d]]
        if d != 0:
            put(("2z", d), s.at[p, pn[d], yl, x, R2, :], st["z2"].at[p, slot[d]], me.dz(d))

    def y1(d):
        got("1y", d)
        s[p, pn[d], yl, :, R1, :] += st["y1"][p, slot[d]]

    def send_1z(e, k):
        put(("1z", e, k), s.at[p, pn[e * k], yl, :, R1, :], st["z1"].at[p, (k - 1) if e == 1 else 3 + k], me.dz(e))

    def hop(k):
        for e in (1, -1):
            if (e, k) == (-1, 4):
                continue
            got("1z", e, k)
            d = e * (k - 1)
            s[p, pn[d], yl, :, R1, :] += st["z1"][p, (k - 1) if e == 1 else 3 + k]
            if k > 1:
                send_1z(e, k - 1)

    def x1():
        for i, d in enumerate((2, 1, -1)):
            put(("1x", d), s.at[p, z, yl, cn[d], R1, :], st["x1"].at[p, i], me.dx(d))

    def done1():
        for d in (2, 1, -1):
            got("1x", d)
        tot = s[p, z, yl, x, R1, :].astype(F32)
        for i in range(3):
            tot = tot + st["x1"][p, i].astype(F32)
        st["fin"][p, 0, R1, :] = tot.astype(BF)

    def done2():
        for d in FAR[:-1]:
            got("2z", d)
        tot = s[p, z, yl, x, R2, :].astype(F32)
        for i in range(7):
            tot = tot + st["z2"][p, i].astype(F32)
        st["fin"][p, 0, R2, :] = tot.astype(BF)

    def across():
        put(("fy",), st["fin"].at[p, 0], st["fin"].at[p, 1], me.dy(2))

    def share():
        got("fy")
        st["own"][m] = (st["fin"][p, 0].astype(F32) + st["fin"][p, 1].astype(F32)) * scale
        put(("fd",), st["own"].at[m], st["own"].at[m], me.mate())

    def last():
        got("fd")

    part = functools.partial
    for d in FAR:
        ev.append((0.0, part(swap, d)))
    for i, d in enumerate(FAR):
        t = 1.5 + 0.4 * i
        ev.append((t, part(join, d)))
        ev.append((t + 3.0, part(xb, d)))
        ev.append((t + 6.0, part(xa, d)))
        ev.append((t + 9.0, part(y2, d)))
        ev.append((t + 3.2, part(y1, d)))
        if d == 4:
            ev.append((t + 3.3, part(send_1z, 1, 4)))
        if d == -3:
            ev.append((t + 3.3, part(send_1z, -1, 3)))
    for k in range(4, 0, -1):
        ev.append((8.0 + 3.0 * (4 - k), part(hop, k)))
    ev.append((17.1, x1))
    ev.append((18.0, done2))
    ev.append((20.0, done1))
    ev.append((20.1, across))
    ev.append((23.0, share))
    ev.append((25.0, last))
    return ev


def order(*lists):
    todo = [(t, n, i, f) for n, evs in enumerate(lists) for i, (t, f) in enumerate(evs)]
    for _, _, _, f in sorted(todo, key=lambda e: e[:3]):
        f()


def later(evs, dt):
    return [(t + dt, f) for t, f in evs]


def dot(a, b, dims):
    return lax.dot_general(a, b, (dims, ((), ())), preferred_element_type=F32)


NN, NT, TN = ((1,), (0,)), ((1,), (1,)), ((0,), (0,))


def kernel(
    x0_h, lin_h, go_h, ra_h, ea_h, rb_h, eb_h,
    gl_h, gb_h, o0, o1, o2, o3,
    w, g, s, dd, xa, xb, y1, y2, z1, z2, x1, fin, own,
    x0, lin, go, mid, gm, ma, mb, ca, gl, gb,
    n16, acc, send, recv, loc,
):
    me = Place()
    mail = Mail(send, recv)
    scale = 1.0 / math.sqrt(256 * TOK)
    st = dict(xa=xa, xb=xb, y1=y1, y2=y2, z1=z1, z2=z2, x1=x1, fin=fin, own=own)

    def local(i, src, dst):
        return pltpu.make_async_copy(src, dst, loc.at[i])

    loads = [local(2, lin_h, lin), local(3, x0_h, x0), local(4, go_h, go)]
    pairs = ((ra_h, ea_h), (eb_h, rb_h))

    def own_copies(c):
        return [local(p, pairs[c][p], w.at[2 * p + c, me.z, me.yl, me.x]) for p in (0, 1)]

    for c in (0, 1):
        @pl.when(me.c == c)
        def _():
            for cp in own_copies(c):
                cp.start()
    for cp in loads:
        cp.start()
    barrier = pltpu.get_barrier_semaphore()
    peers = me.peers()
    for dev in peers:
        pl.semaphore_signal(barrier, inc=1, device_id=dev, device_id_type=pl.DeviceIdType.MESH)
    pl.semaphore_wait(barrier, len(peers))
    for c in (0, 1):
        @pl.when(me.c == c)
        def _():
            for cp in own_copies(c):
                cp.wait()
    for cp in loads:
        cp.wait()

    order(gather_events(me, mail, w, 0), later(gather_events(me, mail, w, 1), 2.0))

    def plane_of(m, i):
        return w[m, i].reshape(PLANE, RANK)

    def columns(i):
        return pl.ds(pl.multiple_of(i * PLANE, PLANE), PLANE)

    def as_plane(v):
        return v.astype(BF).reshape(2, NX, ROWS, RANK)

    acc[...] = jnp.zeros_like(acc)

    @pl.loop(0, NZ)
    def _(i):
        c = columns(i)
        masked = (go[:, c].astype(F32) * x0[:, c].astype(F32)).astype(BF)
        mb[:, c] = masked
        acc[0] += dot(lin[:, c], plane_of(0, i), NN)
        acc[1] += dot(masked, plane_of(1, i), NN)

    n16[0] = acc[0].astype(BF)
    n16[1] = acc[1].astype(BF)
    acc[...] = jnp.zeros_like(acc)

    @pl.loop(0, NZ)
    def _(i):
        c = columns(i)
        base = x0[:, c].astype(F32)
        cross = dot(n16[0], plane_of(2, i), NT)
        middle = (lin[:, c].astype(F32) + base * cross).astype(BF)
        mid[:, c] = middle
        gmid = (go[:, c].astype(F32) + dot(n16[1], plane_of(3, i), NT)).astype(BF)
        gm[:, c] = gmid
        ca[:, c] = cross
        masked = (gmid.astype(F32) * base).astype(BF)
        ma[:, c] = masked
        acc[0] += dot(middle, plane_of(3, i), NN)
        acc[1] += dot(masked, plane_of(2, i), NN)
        g[0, i] = as_plane(dot(middle, n16[1], TN))
        g[1, i] = as_plane(dot(masked, n16[0], TN))

    n16[2] = acc[0].astype(BF)
    n16[3] = acc[1].astype(BF)

    @pl.loop(0, NZ)
    def _(i):
        c = columns(i)
        g[2, i] = as_plane(dot(lin[:, c], n16[3], TN))
        g[3, i] = as_plane(dot(mb[:, c], n16[2], TN))

    def results():
        @pl.loop(0, NZ)
        def _(i):
            c = columns(i)
            gmid = gm[:, c].astype(F32)
            cross = dot(n16[2], plane_of(1, i), NT)
            gb[:, c] = (go[:, c].astype(F32) * cross + gmid * ca[:, c]).astype(BF)
            gl[:, c] = (gmid + dot(n16[3], plane_of(0, i), NT)).astype(BF)

        local(0, gl, gl_h).start()
        local(1, gb, gb_h).start()

    mail2 = mail
    order(
        scatter_events(me, mail2, g, s, dd, st, 0, scale),
        later(scatter_events(me, mail2, g, s, dd, st, 1, scale), 2.0),
        [(3.0, results)],
    )
    for m, o in enumerate((o0, o1, o2, o3)):
        o[...] = own[m]
    local(0, gl, gl_h).wait()
    local(1, gb, gb_h).wait()
    mail.drain()


def on_device(cross_base, layer_in, grad_out, reduce_a, expand_a, reduce_b, expand_b):
    anywhere = pl.BlockSpec(memory_space=pl.ANY)
    vmem = pl.BlockSpec(memory_space=pltpu.VMEM)
    V = pltpu.VMEM
    gl, gb, grb, gea, gra, geb = pl.pallas_call(
        kernel,
        out_shape=[jax.ShapeDtypeStruct((TOK, D), BF)] * 2 + [jax.ShapeDtypeStruct((ROWS, RANK), F32)] * 4,
        in_specs=[anywhere] * 7,
        out_specs=[anywhere] * 2 + [vmem] * 4,
        scratch_shapes=[
            V((4, NZ, 2, NX, ROWS, RANK), BF),
            V((4, NZ, 2, NX, ROWS, RANK), BF),
            V((2, NZ, 2, NX, ROWS, RANK), BF),
            V((2, NZ, 2, NX, ROWS, RANK), BF),
            V((2, 8, 2, 2, HALF, RANK), BF),
            V((2, 8, 2, HALF, RANK), BF),
            V((2, 8, NX, HALF, RANK), BF),
            V((2, 8, HALF, RANK), BF),
            V((2, 7, NX, HALF, RANK), BF),
            V((2, 7, HALF, RANK), BF),
            V((2, 3, HALF, RANK), BF),
            V((2, 2, ROWS, RANK), BF),
            V((4, ROWS, RANK), F32),
        ]
        + [V((TOK, D), BF)] * 7
        + [V((TOK, D), F32), V((TOK, D), BF), V((TOK, D), BF)]
        + [
            V((4, TOK, RANK), BF),
            V((2, TOK, RANK), F32),
            pltpu.SemaphoreType.DMA((288,)),
            pltpu.SemaphoreType.DMA((288,)),
            pltpu.SemaphoreType.DMA((8,)),
        ],
        name="window",
        compiler_params=pltpu.CompilerParams(
            collective_id=0, has_side_effects=True, vmem_limit_bytes=62 * 1024 * 1024
        ),
    )(cross_base, layer_in, grad_out, reduce_a, expand_a, reduce_b, expand_b)
    return (gl, gb, gra, gea, grb, geb)


def solution(mesh):
    tokens, rows = P(("fsdp", "rep"), None), P("fsdp", None)
    return jax.shard_map(
        on_device,
        mesh=mesh,
        in_specs=(tokens,) * 3 + (rows,) * 4,
        out_specs=(tokens,) * 2 + (rows,) * 4,
        check_vma=False,
    )
```

time: 823 us -> 110 us (0.13)
  waiting for transfers between devices: 683 us -> 0 us
  Pallas kernels: 0 us -> 102 us
  starting transfers between devices: 80 us -> 0 us
  matrix products: 24.5 us -> 0 us
  between operations: 14.2 us -> 0.66 us
  other arithmetic: 13.4 us -> 0 us
    all_gather x2 -> x0, waiting for transfers between devices: 557 us -> none  [in_one_piece(): out, at, outs = (lax.all_gather(both, axis, axis=dim, tiled=True), 0, [])]
    all_to_all x4 -> x0, waiting for transfers between devices: 126 us -> none  [the longest x2 119 us: sum_at_owner(): lax.all_to_all(pieces, axis, split_axis=0, concat_axis=0, tiled=True)]
    pallas_call x0 -> x1, Pallas kernels: none -> 102 us  [on_device(): pl.pallas_call(kernel, out_shape=[jax.ShapeDtypeStruct((TOK, D), BF)] * 2...]
    all_to_all x4 -> x0, starting transfers between devices: 79.9 us -> none  [the longest x2 63.4 us: sent_to_all(): return lax.all_to_all(copies, axis, split_axis=0, concat_axis=0, tiled=True)]
    dot_general x12 -> x0, matrix products: 24.5 us -> none  [the longest x4 14.4 us: contract_cols(): lax.dot_general(left, right, (((1,), (1,)), ((), ())), preferred_element_...]
  transfers between devices with their start and end apart: 6 -> 0, of which waited for: 6 -> 0; matrix products, arithmetic and copies ran while one was open for 4% -> 0% of each run, Pallas kernels for 0% -> 0%
where the time goes in v1:
time: 110 us; the launch traced here: 109 us
  Pallas kernels  102 us (93%)
  local copies, waits for them, and re-layouts  6.57 us (6%)
    pallas_call x1, Pallas kernels, on_device(): pl.pallas_call(kernel, out_shape=[jax.ShapeDtypeStruct((TOK, D), BF)] * 2...  102 us
    unnamed x16, local copies, waits for them, and re-layouts  6.57 us

profile of v1, /device:TPU:1, one launch (start us, length us, event | category | flops | bytes accessed | tf_op | source)
XLA Modules:
  0.0 109.3 jit_solution(16092994012628238238)
XLA Ops:
  0.6 102.1 %window.1 = (bf16[128,4096]{1,0:T(8,128)(2,1)}, bf16[128,4096]{1,0:T(8,128)(2,1)}, f32[64,256]{1,0:T(8,128)}, f32[64,256]{1,0:T(8,128)}, f32[64,256]{1,0:T(8,128)}, /*index=5*/f32[64,256]{1,0:T(8,128)}) custom-call(bf16[128,4096]{1,0:T(8,128)(2,1)} %x0_h.1, bf16[128,4096]{1,0:T(8,128)(2,1)} %lin_h.1, bf16[128,4096]{1,0:T(8,128)(2,1)} %go_h.1, ...), custom_call_target="tpu_custom_call" | custom-call | tf_op jit(solution)/shard_map/window/pallas_call | solution.py:453
  102.7 0.0 copy-start
  102.7 2.4 %copy.19 = bf16[128,4096]{1,0:T(8,128)(2,1)} copy(bf16[128,4096]{1,0:T(8,128)(2,1)} %get-tuple-element.24) | data formatting | bytes 2097152
  105.1 0.0 copy-done
  105.1 0.0 copy-start.4
  105.1 1.0 copy.20
  106.1 0.0 copy-done.4
  106.1 0.0 copy-start.3
  106.1 0.6 copy.21
  106.7 0.2 copy-done.3
  107.0 0.0 copy-start.2
  107.0 0.6 copy.22
  107.6 0.2 copy-done.2
  107.8 0.0 copy-start.1
  107.8 0.6 copy.23
  108.5 0.2 copy-done.1
  108.7 0.6 copy.24
Async XLA Ops:
  102.7 2.4 %copy-start = (bf16[128,4096]{1,0:T(8,128)(2,1)S(1)}, bf16[128,4096]{1,0:T(8,128)(2,1)}, u32[]{:S(2)}) copy-start(bf16[128,4096]{1,0:T(8,128)(2,1)} %get-tuple-element.25) | copy-start | bytes 3145732
  105.1 1.0 copy-start.4
  106.1 0.9 copy-start.3
  107.0 0.9 copy-start.2
  107.8 0.9 copy-start.1

commit v2 on v1

--- a/solution.py
+++ b/solution.py
@@ -16,7 +16,6 @@
 NEAR = (0, 1, -1, 2, -2, 3, -3, 4)
 UP = (0, -1, -2, -3)
 R1, R2 = pl.ds(0, HALF), pl.ds(HALF, HALF)
-OUTS = 4
 
 
 class Place:
@@ -45,12 +44,15 @@
     def mate(self):
         return self.at(self.x, self.y, self.z, 1 - self.c)
 
+    def across(self):
+        return self.at(self.x, (self.y + 2) % NY, self.z, 1 - self.c)
+
     def peers(self):
         return (
             [self.dx(d) for d in (1, -1, 2)]
             + [self.dy(d) for d in (1, -1, 2)]
             + [self.dz(d) for d in (1, -1, 2, -2, 3, -3, 4)]
-            + [self.mate()]
+            + [self.mate(), self.across()]
         )
 
 
@@ -82,7 +84,7 @@
             copy.wait_send()
 
 
-def gather_events(me, mail, w, p):
+def gather_events(me, mail, w, p, use, sequence, start, step):
     m = 2 * p + me.c
     pn, cn, z, yl, oyl, x = me.planes, me.cols, me.z, me.yl, me.oyl, me.x
     ev = []
@@ -117,8 +119,9 @@
     def rows():
         for d in (1, -1, 2):
             got("1x", d)
-        for e in (1, -1):
-            same(("1z", e, 1), w.at[m, z, yl, :, R1, :], me.dz(e))
+        for k in (1, 2):
+            for e in (1, -1):
+                same(("1z", e, k), w.at[m, z, yl, :, R1, :], me.dz(k * e))
         send_1y(0)
 
     def zs(k):
@@ -136,15 +139,26 @@
         e = up(d)
         same(("2xb", d), w.at[m, pn[d], :, cn[-e], R2, :], me.dx(e))
 
-    def hop(k):
-        for e in (1, -1):
-            if (e, k) == (-1, 4):
-                continue
-            got("1z", e, k)
-            d = -e * k
-            if k < 3 or (e, k) == (1, 3):
-                same(("1z", e, k + 1), w.at[m, pn[d], yl, :, R1, :], me.dz(e))
-            send_1y(4 if k == 4 else d)
+    def near():
+        for e in (1, -1):
+            got("1z", e, 1)
+            send_1y(-e)
+
+    def relay():
+        for e in (1, -1):
+            got("1z", e, 2)
+            block = w.at[m, pn[-2 * e], yl, :, R1, :]
+            same(("1z", e, 3), block, me.dz(e))
+            if e == 1:
+                same(("1z", e, 4), block, me.dz(2))
+            send_1y(-2 * e)
+
+    def far():
+        for e in (1, -1):
+            got("1z", e, 3)
+            send_1y(-3 * e)
+        got("1z", 1, 4)
+        send_1y(4)
 
     def d1(d):
         got("1y", d)
@@ -154,38 +168,31 @@
         got("2xb", d)
         same(("d2", d), w.at[m, pn[d], :, :, R2, :], me.mate())
 
-    def last():
-        for d in NEAR:
-            got("d1", d)
-            got("d2", d)
-
+    def ready(d):
+        got("d1", -d if abs(d) < 4 else d)
+        got("d2", -d if abs(d) < 4 else d)
+        use(d)
+
+    part = functools.partial
     ev.append((0.0, first))
     ev.append((3.0, rows))
-    ev.append((3.2, functools.partial(zs, 1)))
-    ev.append((3.5, functools.partial(xa, 0)))
-    ev.append((3.9, functools.partial(zs, 2)))
-    ev.append((4.5, functools.partial(zs, 3)))
-    ev.append((5.0, functools.partial(zs, 4)))
     for k in range(1, 5):
-        t = 4.9 + 0.9 * k
-        for d in ((k, -k) if k < 4 else (4,)):
-            ev.append((t, functools.partial(xa, d)))
-    for k in range(0, 5):
-        t = 6.2 + 1.3 * k
-        for d in ((k, -k) if 0 < k < 4 else (k,)):
-            ev.append((t, functools.partial(xb, d)))
-            ev.append((t + 2.6, functools.partial(d2, d)))
-    for k in range(1, 5):
-        ev.append((3.0 + 3.0 * k, functools.partial(hop, k)))
-    for k in range(0, 5):
-        t = 6.0 + 3.0 * k
-        for d in ((k, -k) if 0 < k < 4 else (k,)):
-            ev.append((t, functools.partial(d1, d)))
-    ev.append((20.0, last))
+        ev.append((2.6 + 0.5 * k, part(zs, k)))
+    ev.append((6.1, near))
+    ev.append((6.6, relay))
+    ev.append((9.6, far))
+    for d in NEAR:
+        k = abs(d)
+        ev.append((5.8 + 0.5 * k if k else 3.3, part(xa, d)))
+        ev.append((8.9 + 0.5 * k if k else 6.4, part(xb, d)))
+        ev.append((12.1 + 0.5 * k if k else 9.6, part(d2, d)))
+        ev.append(((6.5, 9.5, 9.8, 12.7, 12.9)[k], part(d1, d)))
+    for i, d in enumerate(sequence):
+        ev.append((start + step * i, part(ready, d)))
     return ev
 
 
-def scatter_events(me, mail, g, s, dd, st, p, scale):
+def scatter_events(me, mail, g, s, dd, st, p, scale, step):
     m, mo = 2 * p + me.c, 2 * p + 1 - me.c
     pn, cn, z, yl, oyl, x = me.planes, me.cols, me.z, me.yl, me.oyl, me.x
     ev = []
@@ -242,19 +249,33 @@
     def y1(d):
         got("1y", d)
         s[p, pn[d], yl, :, R1, :] += st["y1"][p, slot[d]]
+        if d == 4:
+            send_1z(1, 4)
+        elif abs(d) in (1, 3):
+            send_1z(1 if d > 0 else -1, abs(d))
 
     def send_1z(e, k):
-        put(("1z", e, k), s.at[p, pn[e * k], yl, :, R1, :], st["z1"].at[p, (k - 1) if e == 1 else 3 + k], me.dz(e))
-
-    def hop(k):
-        for e in (1, -1):
-            if (e, k) == (-1, 4):
-                continue
-            got("1z", e, k)
-            d = e * (k - 1)
-            s[p, pn[d], yl, :, R1, :] += st["z1"][p, (k - 1) if e == 1 else 3 + k]
-            if k > 1:
-                send_1z(e, k - 1)
+        hops = {1: e, 2: 2 * e, 3: e, 4: 2}[k]
+        put(("1z", e, k), s.at[p, pn[e * k], yl, :, R1, :], st["z1"].at[p, slot1(e, k)], me.dz(hops))
+
+    def slot1(e, k):
+        return k - 1 if e == 1 else 3 + k
+
+    def add1(e, k, d):
+        got("1z", e, k)
+        s[p, pn[d], yl, :, R1, :] += st["z1"][p, slot1(e, k)]
+
+    def meet():
+        add1(1, 4, 2)
+        for e in (1, -1):
+            add1(e, 3, 2 * e)
+            send_1z(e, 2)
+
+    def home():
+        for k in (1, 2):
+            for e in (1, -1):
+                add1(e, k, 0)
+        x1()
 
     def x1():
         for i, d in enumerate((2, 1, -1)):
@@ -277,39 +298,32 @@
         st["fin"][p, 0, R2, :] = tot.astype(BF)
 
     def across():
-        put(("fy",), st["fin"].at[p, 0], st["fin"].at[p, 1], me.dy(2))
+        for i, dev in ((1, me.mate()), (2, me.dy(2)), (3, me.across())):
+            put(("f", i), st["fin"].at[p, 0], st["fin"].at[p, i], dev)
 
     def share():
-        got("fy")
-        st["own"][m] = (st["fin"][p, 0].astype(F32) + st["fin"][p, 1].astype(F32)) * scale
-        put(("fd",), st["own"].at[m], st["own"].at[m], me.mate())
-
-    def last():
-        got("fd")
+        for i in (1, 2, 3):
+            got("f", i)
+        half = [st["fin"][p, i].astype(F32) for i in range(4)]
+        st["own"][m] = (half[0] + half[2]) * scale
+        st["own"][mo] = (half[1] + half[3]) * scale
 
     part = functools.partial
-    for d in FAR:
-        ev.append((0.0, part(swap, d)))
     for i, d in enumerate(FAR):
-        t = 1.5 + 0.4 * i
+        t = step * i
         ev.append((t, part(join, d)))
         ev.append((t + 3.0, part(xb, d)))
         ev.append((t + 6.0, part(xa, d)))
         ev.append((t + 9.0, part(y2, d)))
         ev.append((t + 3.2, part(y1, d)))
-        if d == 4:
-            ev.append((t + 3.3, part(send_1z, 1, 4)))
-        if d == -3:
-            ev.append((t + 3.3, part(send_1z, -1, 3)))
-    for k in range(4, 0, -1):
-        ev.append((8.0 + 3.0 * (4 - k), part(hop, k)))
-    ev.append((17.1, x1))
-    ev.append((18.0, done2))
-    ev.append((20.0, done1))
-    ev.append((20.1, across))
-    ev.append((23.0, share))
-    ev.append((25.0, last))
-    return ev
+    end = step * 7
+    ev.append((end + 3.4, meet))
+    ev.append((end + 6.6, home))
+    ev.append((end + 9.9, done1))
+    ev.append((end + 12.5, done2))
+    ev.append((end + 12.6, across))
+    ev.append((end + 15.6, share))
+    return ev, swap
 
 
 def order(*lists):
@@ -331,9 +345,9 @@
 
 def kernel(
     x0_h, lin_h, go_h, ra_h, ea_h, rb_h, eb_h,
-    gl_h, gb_h, o0, o1, o2, o3,
+    big_h, small,
     w, g, s, dd, xa, xb, y1, y2, z1, z2, x1, fin, own,
-    x0, lin, go, mid, gm, ma, mb, ca, gl, gb,
+    x0, lin, go, gm, mb, ca, big,
     n16, acc, send, recv, loc,
 ):
     me = Place()
@@ -367,10 +381,6 @@
         def _():
             for cp in own_copies(c):
                 cp.wait()
-    for cp in loads:
-        cp.wait()
-
-    order(gather_events(me, mail, w, 0), later(gather_events(me, mail, w, 1), 2.0))
 
     def plane_of(m, i):
         return w[m, i].reshape(PLANE, RANK)
@@ -381,68 +391,72 @@
     def as_plane(v):
         return v.astype(BF).reshape(2, NX, ROWS, RANK)
 
-    acc[...] = jnp.zeros_like(acc)
-
-    @pl.loop(0, NZ)
-    def _(i):
+    rs0, swap0 = scatter_events(me, mail, g, s, dd, st, 0, scale, 0.7)
+    rs1, swap1 = scatter_events(me, mail, g, s, dd, st, 1, scale, 0.4)
+
+    def loaded():
+        for cp in loads:
+            cp.wait()
+        acc[...] = jnp.zeros_like(acc)
+
+    def enter(d):
+        i = me.planes[d]
         c = columns(i)
         masked = (go[:, c].astype(F32) * x0[:, c].astype(F32)).astype(BF)
         mb[:, c] = masked
         acc[0] += dot(lin[:, c], plane_of(0, i), NN)
         acc[1] += dot(masked, plane_of(1, i), NN)
 
-    n16[0] = acc[0].astype(BF)
-    n16[1] = acc[1].astype(BF)
-    acc[...] = jnp.zeros_like(acc)
-
-    @pl.loop(0, NZ)
-    def _(i):
+    def narrow(a):
+        n16[a] = acc[0].astype(BF)
+        n16[a + 1] = acc[1].astype(BF)
+        acc[...] = jnp.zeros_like(acc)
+
+    def middle(d):
+        i = me.planes[d]
         c = columns(i)
         base = x0[:, c].astype(F32)
         cross = dot(n16[0], plane_of(2, i), NT)
-        middle = (lin[:, c].astype(F32) + base * cross).astype(BF)
-        mid[:, c] = middle
+        mid = (lin[:, c].astype(F32) + base * cross).astype(BF)
         gmid = (go[:, c].astype(F32) + dot(n16[1], plane_of(3, i), NT)).astype(BF)
         gm[:, c] = gmid
         ca[:, c] = cross
         masked = (gmid.astype(F32) * base).astype(BF)
-        ma[:, c] = masked
-        acc[0] += dot(middle, plane_of(3, i), NN)
+        g[0, i] = as_plane(dot(mid, n16[1], TN))
+        g[1, i] = as_plane(dot(masked, n16[0], TN))
+        swap0(-d if d != 4 else d)
+        acc[0] += dot(mid, plane_of(3, i), NN)
         acc[1] += dot(masked, plane_of(2, i), NN)
-        g[0, i] = as_plane(dot(middle, n16[1], TN))
-        g[1, i] = as_plane(dot(masked, n16[0], TN))
-
-    n16[2] = acc[0].astype(BF)
-    n16[3] = acc[1].astype(BF)
-
-    @pl.loop(0, NZ)
-    def _(i):
+
+    def outer(d):
+        i = me.planes[d]
         c = columns(i)
         g[2, i] = as_plane(dot(lin[:, c], n16[3], TN))
         g[3, i] = as_plane(dot(mb[:, c], n16[2], TN))
-
-    def results():
-        @pl.loop(0, NZ)
-        def _(i):
-            c = columns(i)
-            gmid = gm[:, c].astype(F32)
-            cross = dot(n16[2], plane_of(1, i), NT)
-            gb[:, c] = (go[:, c].astype(F32) * cross + gmid * ca[:, c]).astype(BF)
-            gl[:, c] = (gmid + dot(n16[3], plane_of(0, i), NT)).astype(BF)
-
-        local(0, gl, gl_h).start()
-        local(1, gb, gb_h).start()
-
-    mail2 = mail
+        swap1(-d if d != 4 else d)
+
+    def result(i):
+        c = pl.ds(i * PLANE, PLANE)
+        gmid = gm[:, c].astype(F32)
+        cross = dot(n16[2], plane_of(1, i), NT)
+        big[1, :, c] = (go[:, c].astype(F32) * cross + gmid * ca[:, c]).astype(BF)
+        big[0, :, c] = (gmid + dot(n16[3], plane_of(0, i), NT)).astype(BF)
+
+    def write():
+        local(0, big, big_h).start()
+
+    part = functools.partial
     order(
-        scatter_events(me, mail2, g, s, dd, st, 0, scale),
-        later(scatter_events(me, mail2, g, s, dd, st, 1, scale), 2.0),
-        [(3.0, results)],
+        gather_events(me, mail, w, 0, enter, NEAR, 13.0, 0.5),
+        later(gather_events(me, mail, w, 1, middle, FAR, 15.4, 0.7), 3.0),
+        [(12.9, loaded), (17.0, part(narrow, 0)), (24.1, part(narrow, 2))],
+        [(24.2 + 0.4 * i, part(outer, d)) for i, d in enumerate(FAR)],
+        later(rs0, 20.0),
+        later(rs1, 26.0),
+        [(29.5 + 1.0 * i, part(result, i)) for i in range(NZ)] + [(37.6, write)],
     )
-    for m, o in enumerate((o0, o1, o2, o3)):
-        o[...] = own[m]
-    local(0, gl, gl_h).wait()
-    local(1, gb, gb_h).wait()
+    small[...] = own[...]
+    local(0, big, big_h).wait()
     mail.drain()
 
 
@@ -450,11 +464,11 @@
     anywhere = pl.BlockSpec(memory_space=pl.ANY)
     vmem = pl.BlockSpec(memory_space=pltpu.VMEM)
     V = pltpu.VMEM
-    gl, gb, grb, gea, gra, geb = pl.pallas_call(
+    big, small = pl.pallas_call(
         kernel,
-        out_shape=[jax.ShapeDtypeStruct((TOK, D), BF)] * 2 + [jax.ShapeDtypeStruct((ROWS, RANK), F32)] * 4,
+        out_shape=[jax.ShapeDtypeStruct((2, TOK, D), BF), jax.ShapeDtypeStruct((4, ROWS, RANK), F32)],
         in_specs=[anywhere] * 7,
-        out_specs=[anywhere] * 2 + [vmem] * 4,
+        out_specs=[anywhere, vmem],
         scratch_shapes=[
             V((4, NZ, 2, NX, ROWS, RANK), BF),
             V((4, NZ, 2, NX, ROWS, RANK), BF),
@@ -467,11 +481,11 @@
             V((2, 7, NX, HALF, RANK), BF),
             V((2, 7, HALF, RANK), BF),
             V((2, 3, HALF, RANK), BF),
-            V((2, 2, ROWS, RANK), BF),
+            V((2, 4, ROWS, RANK), BF),
             V((4, ROWS, RANK), F32),
         ]
-        + [V((TOK, D), BF)] * 7
-        + [V((TOK, D), F32), V((TOK, D), BF), V((TOK, D), BF)]
+        + [V((TOK, D), BF)] * 5
+        + [V((TOK, D), F32), V((2, TOK, D), BF)]
         + [
             V((4, TOK, RANK), BF),
             V((2, TOK, RANK), F32),
@@ -484,7 +498,7 @@
             collective_id=0, has_side_effects=True, vmem_limit_bytes=62 * 1024 * 1024
         ),
     )(cross_base, layer_in, grad_out, reduce_a, expand_a, reduce_b, expand_b)
-    return (gl, gb, gra, gea, grb, geb)
+    return (big[0], big[1], small[2], small[1], small[0], small[3])
 
 
 def solution(mesh):

time: 110 us -> 90.9 us (0.83)
  Pallas kernels: 102 us -> 86.4 us
  local copies, waits for them, and re-layouts: 6.57 us -> 3.82 us
    pallas_call x1, Pallas kernels: 102 us -> 86.4 us  [on_device(): pl.pallas_call(kernel, out_shape=[jax.ShapeDtypeStruct((2, TOK, D), BF),...]
    unnamed x16 -> x2, local copies, waits for them, and re-layouts: 6.57 us -> 0.01 us
    squeeze x0 -> x2, local copies, waits for them, and re-layouts: none -> 3.82 us  [on_device(): return (big[0], big[1], small[2], small[1], small[0], small[3])]
where the time goes in v2:
time: 90.9 us; the launch traced here: 90.8 us
  Pallas kernels  86.4 us (95%)
  local copies, waits for them, and re-layouts  3.82 us (4%)
    pallas_call x1, Pallas kernels, on_device(): pl.pallas_call(kernel, out_shape=[jax.ShapeDtypeStruct((2, TOK, D), BF),...  86.4 us
    squeeze x2, local copies, waits for them, and re-layouts, on_device(): return (big[0], big[1], small[2], small[1], small[0], small[3])  3.82 us

profile of v2, /device:TPU:1, one launch (start us, length us, event | category | flops | bytes accessed | tf_op | source)
XLA Modules:
  0.0 90.8 jit_solution(931670376074081420)
XLA Ops:
  0.6 86.4 %window.1 = (bf16[2,128,4096]{2,1,0:T(8,128)(2,1)}, f32[4,64,256]{2,1,0:T(8,128)}) custom-call(bf16[128,4096]{1,0:T(8,128)(2,1)} %x0_h.1, bf16[128,4096]{1,0:T(8,128)(2,1)} %lin_h.1, bf16[128,4096]{1,0:T(8,128)(2,1)} %go_h.1, bf16[64,256]{1,0:T(8,128)(2,1)} %ra_h.1, bf16[64,256]{1,0:T(8,128)(2,1)} %ea_h.1, bf16[64,256]{1,0:T(8,128)(2,1)} %rb_h.1, ...), custom_call_target="tpu_custom_call" | custom-call | tf_op jit(solution)/shard_map/window/pallas_call | solution.py:467
  87.0 0.0 copy-start
  87.0 3.1 %slice_bitcast_fusion = (bf16[128,4096]{1,0:T(8,128)(2,1)}, bf16[128,4096]{1,0:T(8,128)(2,1)}) fusion(bf16[2,128,4096]{2,1,0:T(8,128)(2,1)} %get-tuple-element.8), kind=kLoop, calls=%fused_computation | loop fusion | bytes 4194304 | tf_op jit(solution)/shard_map/squeeze | solution.py:501
  90.1 0.0 copy-done
  90.1 0.7 slice_bitcast_fusion.2
Async XLA Ops:
  87.0 3.1 %copy-start = (f32[4,64,256]{2,1,0:T(8,128)S(1)}, f32[4,64,256]{2,1,0:T(8,128)}, u32[]{:S(2)}) copy-start(f32[4,64,256]{2,1,0:T(8,128)} %get-tuple-element.9) | copy-start | bytes 786436
